TPU v7x, 32 devices: a whole 2x2x4 slice. The times are simulated.
32 devices in a mesh: grp: 2 (over x), seq: 16 (over z, y, core).
Axes of the slice: x: 2, y: 2, z: 4, core: 2. Of those that a mesh axis runs over, the one named last changes fastest.
Arguments:
- llm_grad: bfloat16 [4096, 8192], P('seq', 'grp'), may hold values from -6 to 6
- image_grid: int32 [256, 2], replicated, may hold values from 1 to 3, as said below
- image_owner: int32 [256], replicated, may hold values from 0 to 15, as said below
- row_start: int32 [256], replicated, may hold values from 0 to 255, as said below
- merger_pre: bfloat16 [48, 16, 2560], P(None, 'seq', 'grp'), may hold values from -6 to 6
- vit_out: bfloat16 [192, 16, 1280], P(None, 'seq'), may hold values from -6 to 6
- vit_pre: bfloat16 [192, 16, 2560], P(None, 'seq', 'grp'), may hold values from -6 to 6
- ln_gain: float32 [1280], replicated, may hold values from 0.25 to 1.75
- merger_out_w: bfloat16 [8192, 2560], P('seq', 'grp'), may hold values from -0.0625 to 0.0625
- merger_in_w: bfloat16 [2560, 5120], P('grp', 'seq'), may hold values from -0.125 to 0.125
- vit_fc2_w: bfloat16 [1280, 2560], P('seq', 'grp'), may hold values from -0.15625 to 0.15625
Outputs:
- patch_grad: bfloat16 [192, 16, 1280], P('grp', 'seq')
- fc1_grad: bfloat16 [192, 16, 2560], P(None, 'seq', 'grp')
- fc2_w_grad: float32 [1280, 2560], P('seq', 'grp')
Inputs may be any that keep to these rules, and one draw needn't show every extreme that they name: `image_grid`: height times width is 1 to 3; the first image of every shard is 1 by 3; the last image of shard 0 is 1 by 1. `image_owner`: the 16 images of one shard have 16 different owners. An image's rows row_start to row_start + t - 1 lie inside its shard and meet no other image's rows; a shard's images follow the order of k; the last image of every shard ends at the shard's last row; the first image of shard 0 starts at row 0.
All inputs are finite; a program needn't handle non-finite values.
Results may differ from a plain program's by a relative error of at most 0.02.
Values may be sent and summed in bfloat16 or wider, within the bound.
A program may use at most 128 MiB of HBM per device.

v0:
```python
import jax
import jax.numpy as jnp
from jax import lax
from jax.sharding import PartitionSpec as P

SLOT = 3


def gelu_slope(values):
    return (
        0.5 * (1.0 + lax.erf(values * 0.7071067811865476))
        + values * jnp.exp(-0.5 * values * values) * 0.3989422804014327
    )


def patch_table(widths, counts, slots):
    places = jnp.arange(4 * slots, dtype=jnp.int32)
    merged = places // 4
    corner = places % 4
    row_in = merged[None, :] // widths[:, None]
    col_in = merged[None, :] % widths[:, None]
    target = (
        (2 * row_in + corner[None, :] // 2) * (2 * widths[:, None])
        + 2 * col_in
        + corner[None, :] % 2
    )
    usable = merged[None, :] < counts[:, None]
    return ((target[:, None, :] == places[None, :, None]) & usable[:, None, :]).astype(jnp.float32)


def norm_backward(upstream, inputs, scales):
    average = jnp.mean(inputs, -1, keepdims=True)
    centred = inputs - average
    inverse_std = lax.rsqrt(jnp.mean(centred * centred, -1, keepdims=True) + 1e-06)
    normed = centred * inverse_std
    scaled = upstream * scales
    return inverse_std * (
        scaled
        - jnp.mean(scaled, -1, keepdims=True)
        - normed * jnp.mean(scaled * normed, -1, keepdims=True)
    )


def on_device(
    llm_grad,
    image_grid,
    image_owner,
    row_start,
    merger_pre,
    vit_out,
    vit_pre,
    ln_gain,
    merger_out_w,
    merger_in_w,
    vit_fc2_w,
):
    seq_count = lax.axis_size("seq")
    own_index = lax.axis_index("seq")
    grids = image_grid.reshape(seq_count, seq_count, 2)
    counts = grids[:, :, 0] * grids[:, :, 1]
    widths = grids[:, :, 1]
    owners = image_owner.reshape(seq_count, seq_count)
    starts = row_start.reshape(seq_count, seq_count)
    within = jnp.arange(SLOT, dtype=jnp.int32)
    peers = jnp.arange(seq_count, dtype=jnp.int32)
    shard_rows = llm_grad.shape[0]
    my_owners = lax.dynamic_index_in_dim(owners, own_index, 0, keepdims=False)
    my_counts = lax.dynamic_index_in_dim(counts, own_index, 0, keepdims=False)
    my_starts = lax.dynamic_index_in_dim(starts, own_index, 0, keepdims=False)
    targets = (my_owners[None, :] == peers[:, None]).astype(jnp.int32)
    send_counts = jnp.sum(targets * my_counts[None, :], 1)
    send_starts = jnp.sum(targets * my_starts[None, :], 1)
    indices = jnp.minimum(send_starts[:, None] + within[None, :], shard_rows - 1)
    usable = within[None, :] < send_counts[:, None]
    picked = jnp.take(llm_grad, indices.reshape(-1), axis=0)
    outgoing = jnp.where(usable.reshape(-1, 1), picked, jnp.zeros_like(picked)).reshape(
        seq_count, SLOT, llm_grad.shape[1]
    )
    received = (owners == own_index).astype(jnp.int32)
    recv_counts = jnp.sum(received * counts, 1)
    recv_widths = jnp.sum(received * widths, 1)
    wide_rows = lax.all_gather(outgoing, "grp", axis=2, tiled=True)
    flat = wide_rows.reshape(-1, wide_rows.shape[2])
    columns = flat
    folded = jnp.dot(
        columns,
        lax.all_gather(merger_out_w, "seq", axis=0, tiled=True),
        preferred_element_type=jnp.float32,
    )
    source_grad = folded.astype(jnp.bfloat16).reshape(seq_count, SLOT, merger_out_w.shape[1])
    arrived = lax.all_to_all(source_grad, "seq", split_axis=0, concat_axis=0, tiled=True)
    unit_grad = arrived.reshape(seq_count * SLOT, merger_out_w.shape[1])
    pre_act = merger_pre[:, 0, :].astype(jnp.float32)
    pre_grad = (gelu_slope(pre_act) * unit_grad.astype(jnp.float32)).astype(jnp.bfloat16)
    merged_part = jnp.dot(
        pre_grad,
        lax.all_gather(merger_in_w, "seq", axis=1, tiled=True),
        preferred_element_type=jnp.float32,
    )
    vit_width = vit_out.shape[2]
    table = patch_table(recv_widths, recv_counts, SLOT)
    patch_part = jnp.einsum(
        "spq,sqc->spc",
        table,
        merged_part.reshape(seq_count, 4 * SLOT, vit_width),
        precision=lax.Precision.HIGHEST,
    ).reshape(-1, vit_width)
    patch_in = lax.psum(patch_part.astype(jnp.bfloat16), "grp").astype(jnp.float32)
    patch_grad = norm_backward(patch_in, vit_out[:, 0, :].astype(jnp.float32), ln_gain).astype(
        jnp.bfloat16
    )
    group_rows = patch_grad.shape[0] // lax.axis_size("grp")
    own_rows = lax.dynamic_slice_in_dim(
        patch_grad, lax.axis_index("grp") * group_rows, group_rows, 0
    )
    columns = patch_grad
    act_grad = jnp.dot(
        columns,
        lax.all_gather(vit_fc2_w, "seq", axis=0, tiled=True),
        preferred_element_type=jnp.float32,
    )
    fc_in = vit_pre[:, 0, :].astype(jnp.float32)
    sigmoid_q = jax.nn.sigmoid(1.702 * fc_in)
    activation = (fc_in * sigmoid_q).astype(jnp.bfloat16)
    fc1_grad = ((sigmoid_q + 1.702 * fc_in * sigmoid_q * (1.0 - sigmoid_q)) * act_grad).astype(
        jnp.bfloat16
    )
    columns = patch_grad
    weight_grad = lax.psum_scatter(
        lax.dot_general(
            columns, activation, (((0,), (0,)), ((), ())), preferred_element_type=jnp.float32
        ),
        "seq",
        scatter_dimension=0,
        tiled=True,
    )
    return (
        own_rows.reshape(group_rows, 1, vit_width),
        fc1_grad.reshape(-1, 1, vit_pre.shape[2]),
        weight_grad,
    )


def solution(mesh):
    return jax.shard_map(
        on_device,
        mesh=mesh,
        in_specs=(
            P("seq", "grp"),
            P(),
            P(),
            P(),
            P(None, "seq", "grp"),
            P(None, "seq", None),
            P(None, "seq", "grp"),
            P(),
            P("seq", "grp"),
            P("grp", "seq"),
            P("seq", "grp"),
        ),
        out_specs=(P("grp", "seq", None), P(None, "seq", "grp"), P("seq", "grp")),
        check_vma=False,
    )
```

profile of v0, /device:TPU:0, one launch (start us, length us, event | category | flops | bytes accessed | tf_op | source)
XLA Modules:
  0.0 416.5 jit_solution(1489986869144480326)
XLA Ops:
  7.2 0.0 copy-start
  7.2 0.0 all-gather.4.cloned.1.call-start
  7.2 0.7 all-gather.4.cloned.1.call-update
  7.9 0.0 all-gather.6.cloned.1.call-start
  8.0 0.7 all-gather.6.cloned.1.call-update
  8.7 0.8 reshape.409
  9.4 0.8 reshape.410
  10.2 0.8 reshape.411
  11.0 0.1 select_reduce_fusion.2
  11.1 0.1 select_reduce_fusion.1
  11.2 0.1 add_minimum_fusion
  11.3 0.1 min.22
  11.4 0.0 copy-done
  11.4 0.8 gather_fusion
  12.2 0.2 gather.7
  12.4 0.1 compare_and_fusion
  12.5 0.1 iota_compare_fusion.2
  12.6 0.4 select_select_fusion
  13.0 15.6 %all_gather.12 = bf16[16,3,8192]{2,1,0:T(4,128)(2,1)} all-gather(bf16[16,3,4096]{2,1,0:T(4,128)(2,1)S(1)} %select_select_fusion), channel_id=1, replica_groups=mesh['grp'=2,'seq'=16] {'grp'}, dimensions={2}, use_global_device_ids=true | all-gather | bytes 1179648 | tf_op jit(solution)/shard_map/all_gather | solution.py:82
  28.7 1.8 reshape.412
  30.6 0.1 broadcast_compare_fusion
  30.6 0.0 copy-start.3
  30.6 90.5 %all-gather.4.cloned.1.call-done = bf16[8192,1280]{1,0:T(8,128)(2,1)} async-done(((bf16[512,1280]{1,0:T(8,128)(2,1)}), bf16[8192,1280]{1,0:T(8,128)(2,1)}) %all-gather.4.cloned.1.call-update) | async-done | bytes 20971536 | tf_op jit(solution)/shard_map/all_gather | solution.py:87
  121.1 8.9 %convolution_convert_fusion.1 = bf16[48,1280]{1,0:T(8,128)(2,1)S(1)} fusion(bf16[48,8192]{1,0:T(8,128)(2,1)S(1)} %reshape.412, bf16[8192,1280]{1,0:T(8,128)(2,1)} %all-gather.4.cloned.1.call-done), kind=kOutput, calls=%fused_computation.5 | convolution fusion | flops 1006694400 | bytes 21880832 | tf_op jit(solution)/shard_map/dot_general | solution.py:85
  130.0 0.7 reshape.413
  130.7 4.7 %all-to-all-start = ((bf16[16,3,1280]{2,1,0:T(4,128)(2,1)}), bf16[16,3,1280]{2,1,0:T(4,128)(2,1)S(1)}, u32[]{:S(2)}, u32[]{:S(2)}) async-start(bf16[16,3,1280]{2,1,0:T(4,128)(2,1)} %reshape.413), calls=%async_computation | async-start | bytes 327680 | tf_op jit(solution)/shard_map/all_to_all | solution.py:91
  135.4 0.0 all-reduce.2.cloned.1.call-start
  135.5 0.3 fusion.50
  135.7 11.2 %all-to-all-done = bf16[16,3,1280]{2,1,0:T(4,128)(2,1)S(1)} async-done(((bf16[16,3,1280]{2,1,0:T(4,128)(2,1)}), bf16[16,3,1280]{2,1,0:T(4,128)(2,1)S(1)}, u32[]{:S(2)}, u32[]{:S(2)}) %all-to-all-start) | async-done | bytes 122912 | tf_op jit(solution)/shard_map/all_to_all | solution.py:91
  146.9 0.1 reshape.418
  147.0 83.6 %all-gather.6.cloned.1.call-done = bf16[1280,5120]{0,1:T(8,128)(2,1)} async-done(((bf16[1280,320]{0,1:T(8,128)(2,1)}), bf16[1280,5120]{0,1:T(8,128)(2,1)}) %all-gather.6.cloned.1.call-update) | async-done | bytes 13107216 | tf_op jit(solution)/shard_map/all_gather | solution.py:97
  230.6 0.0 copy-done.3
  230.6 9.6 %fusion.36 = f32[48,5120]{1,0:T(8,128)} fusion(bf16[1280,5120]{0,1:T(8,128)(2,1)} %all-gather.6.cloned.1.call-done, f32[48,1280]{1,0:T(8,128)S(1)} %reshape.418, bf16[48,1,1280]{2,0,1:T(8,128)(2,1)S(1)} %copy-done.3), kind=kOutput, calls=%fused_computation.50 | convolution fusion | flops 629821440 | bytes 14458880 | tf_op jit(solution)/shard_map/dot_general | solution.py:95
  240.2 0.0 copy-start.1
  240.2 0.0 copy-start.4
  240.2 2.6 reshape.414
  242.8 2.1 convolution_convert_fusion
  244.9 0.9 convert_element_type.60
  245.8 0.0 all-reduce.2.cloned.1.call-update
  245.8 0.0 all-gather.8.cloned.1.call-start
  245.8 0.5 all-gather.8.cloned.1.call-update
  246.4 0.0 reduce-scatter.2.cloned.1.call-start
  246.4 0.0 copy-done.1
  246.4 0.1 convert_reduce_fusion
  246.6 0.3 fusion.18
  246.9 25.3 %all-reduce.2.cloned.1.call-done = bf16[192,1280]{1,0:T(8,128)(2,1)} async-done(((bf16[192,1280]{1,0:T(8,128)(2,1)}), bf16[192,1280]{1,0:T(8,128)(2,1)}) %all-reduce.2.cloned.1.call-update) | async-done | bytes 491536 | tf_op jit(solution)/shard_map/psum | solution.py:108
  272.1 0.0 copy-done.4
  272.1 1.4 fusion.20
  273.5 1.4 fusion.17
  274.9 4.8 %fusion.21 = f32[1280,1280]{1,0:T(8,128)} fusion(bf16[192,1280]{1,0:T(8,128)(2,1)S(1)} %fusion.17, bf16[192,1,1280]{2,0,1:T(8,128)(2,1)} %param.17), kind=kOutput, calls=%fused_computation.31 | convolution fusion | flops 630865920 | bytes 7536640 | tf_op jit(solution)/shard_map/dot_general | solution.py:130
  279.8 0.0 copy-start.2
  279.8 0.0 reduce-scatter.2.cloned.1.call-update
  279.8 0.7 dynamic-slice_bitcast_fusion
  280.5 39.8 %all-gather.8.cloned.1.call-done = bf16[1280,1280]{1,0:T(8,128)(2,1)} async-done(((bf16[80,1280]{1,0:T(8,128)(2,1)}), bf16[1280,1280]{1,0:T(8,128)(2,1)}) %all-gather.8.cloned.1.call-update) | async-done | bytes 3276816 | tf_op jit(solution)/shard_map/all_gather | solution.py:119
  320.4 0.0 copy-done.2
  320.4 3.6 fusion.1
  323.9 86.0 %reduce-scatter.2.cloned.1.call-done = f32[80,1280]{1,0:T(8,128)} async-done(((f32[1280,1280]{1,0:T(8,128)}), f32[80,1280]{1,0:T(8,128)}) %reduce-scatter.2.cloned.1.call-update) | async-done | bytes 409616 | tf_op jit(solution)/shard_map/reduce_scatter | solution.py:129
  (12 shorter events, 0.1 us)
Async XLA Ops:
  7.2 4.2 %copy-start = (bf16[256,4096]{1,0:T(8,128)(2,1)S(1)}, bf16[256,4096]{1,0:T(8,128)(2,1)}, u32[]{:S(2)}) copy-start(bf16[256,4096]{1,0:T(8,128)(2,1)} %param.11) | copy-start | bytes 6291460
  7.2 113.9 %all-gather.4.cloned.1.call-start = ((), (), s32[]{:S(2)}) async-start(), calls=%async_computation.2 | async-start | bytes 22282240 | tf_op jit(solution)/shard_map/all_gather | solution.py:87
  7.9 222.7 %all-gather.6.cloned.1.call-start = ((), (), s32[]{:S(2)}) async-start(), calls=%async_computation.3 | async-start | bytes 13926400 | tf_op jit(solution)/shard_map/all_gather | solution.py:97
  30.6 200.0 %copy-start.3 = (bf16[48,1,1280]{2,0,1:T(8,128)(2,1)S(1)}, bf16[48,1,1280]{2,0,1:T(8,128)(2,1)}, u32[]{:S(2)}) copy-start(bf16[48,1,1280]{2,0,1:T(8,128)(2,1)} %param.15) | copy-start | bytes 368644
  130.7 16.2 %all-to-all-start = ((bf16[16,3,1280]{2,1,0:T(4,128)(2,1)}), bf16[16,3,1280]{2,1,0:T(4,128)(2,1)S(1)}, u32[]{:S(2)}, u32[]{:S(2)}) async-start(bf16[16,3,1280]{2,1,0:T(4,128)(2,1)} %reshape.413), calls=%async_computation | async-start | bytes 327680 | tf_op jit(solution)/shard_map/all_to_all | solution.py:91
  135.4 136.7 %all-reduce.2.cloned.1.call-start = ((), (), s32[]{:S(2)}) async-start(), calls=%async_computation.4 | async-start | bytes 983040 | tf_op jit(solution)/shard_map/psum | solution.py:108
  240.2 6.2 %copy-start.1 = (bf16[192,1,1280]{2,0,1:T(8,128)(2,1)S(1)}, bf16[192,1,1280]{2,0,1:T(8,128)(2,1)}, u32[]{:S(2)}) copy-start(bf16[192,1,1280]{2,0,1:T(8,128)(2,1)} %param.16) | copy-start | bytes 1474564
  240.2 31.9 %copy-start.4 = (f32[1280]{0:T(1024)S(1)}, f32[1280]{0:T(1024)}, u32[]{:S(2)}) copy-start(f32[1280]{0:T(1024)} %param.18) | copy-start | bytes 15364
  245.8 74.6 %all-gather.8.cloned.1.call-start = ((), (), s32[]{:S(2)}) async-start(), calls=%async_computation.5 | async-start | bytes 3481600 | tf_op jit(solution)/shard_map/all_gather | solution.py:119
  246.4 163.6 %reduce-scatter.2.cloned.1.call-start = ((), (), s32[]{:S(2)}) async-start(), calls=%async_computation.6 | async-start | bytes 6963200 | tf_op jit(solution)/shard_map/reduce_scatter | solution.py:129
  279.8 40.6 %copy-start.2 = (bf16[192,1,1280]{2,0,1:T(8,128)(2,1)S(1)}, bf16[192,1,1280]{2,0,1:T(8,128)(2,1)}, u32[]{:S(2)}) copy-start(bf16[192,1,1280]{2,0,1:T(8,128)(2,1)} %param.17) | copy-start | bytes 1474564
Sparse Core Ops, SparseCore 0:
  9.6 111.4 all-gather.3
  123.4 107.1 all-gather.5
  245.9 26.1 all-reduce.1
  274.3 46.0 all-gather.7
  324.8 85.1 reduce-scatter.1
where the time goes:
time: 417 us; the launch traced here: 416 us
  waiting for transfers between devices  338 us (81%)
  matrix products  29 us (7%)
  blocking collectives  15.6 us (4%)
  between operations  14 us (3%)
  local copies, waits for them, and re-layouts  10.3 us (2%)
  starting transfers between devices  4.9 us (1%)
  other arithmetic  4.46 us (1%)
    all_gather x1, waiting for transfers between devices, on_device(): lax.all_gather(merger_out_w, 'seq', axis=0, tiled=True)  90.5 us
    reduce_scatter x1, waiting for transfers between devices, on_device(): lax.psum_scatter(lax.dot_general(columns, activation, (((0,), (0,)), ((),...  86 us
    all_gather x1, waiting for transfers between devices, on_device(): lax.all_gather(merger_in_w, 'seq', axis=1, tiled=True)  83.6 us
    all_gather x1, waiting for transfers between devices, on_device(): lax.all_gather(vit_fc2_w, 'seq', axis=0, tiled=True)  39.8 us
    psum x1, waiting for transfers between devices, on_device(): lax.psum(patch_part.astype(jnp.bfloat16), 'grp').astype(jnp.float32)  25.3 us
    all_gather x1, blocking collectives, on_device(): wide_rows = lax.all_gather(outgoing, 'grp', axis=2, tiled=True)  15.6 us
    all_to_all x1, waiting for transfers between devices, on_device(): lax.all_to_all(source_grad, 'seq', split_axis=0, concat_axis=0, tiled=True)  11.2 us
    dot_general x1, matrix products, on_device(): jnp.dot(pre_grad, lax.all_gather(merger_in_w, 'seq', axis=1, tiled=True),...  9.61 us
  transfers between devices with their start and end apart: 6, of which 6 were waited for; matrix products, arithmetic and copies ran while one was open for 7% of the time, Pallas kernels for 0%

commit v1 on v0

--- a/solution.py
+++ b/solution.py
@@ -105,7 +105,9 @@
         merged_part.reshape(seq_count, 4 * SLOT, vit_width),
         precision=lax.Precision.HIGHEST,
     ).reshape(-1, vit_width)
-    patch_in = lax.psum(patch_part.astype(jnp.bfloat16), "grp").astype(jnp.float32)
+    patch_in = jnp.sum(lax.all_gather(patch_part.astype(jnp.bfloat16), "grp"), axis=0).astype(
+        jnp.float32
+    )
     patch_grad = norm_backward(patch_in, vit_out[:, 0, :].astype(jnp.float32), ln_gain).astype(
         jnp.bfloat16
     )

time: 417 us -> 374 us (0.90)
  waiting for transfers between devices: 338 us -> 276 us
  blocking collectives: 15.6 us -> 34.3 us
    all_gather x1, waiting for transfers between devices: 39.8 us -> 3.82 us  [on_device(): lax.all_gather(vit_fc2_w, 'seq', axis=0, tiled=True)]
    psum x1 -> x0, waiting for transfers between devices: 25.3 us -> none  [on_device(): lax.psum(patch_part.astype(jnp.bfloat16), 'grp').astype(jnp.float32)]
    all_gather x0 -> x1, blocking collectives: none -> 18.7 us  [on_device(): lax.all_gather(patch_part.astype(jnp.bfloat16), 'grp')]
  transfers between devices with their start and end apart: 6 -> 5, of which waited for: 6 -> 5; matrix products, arithmetic and copies ran while one was open for 7% -> 12% of each run, Pallas kernels for 0% -> 0%
where the time goes in v1:
time: 374 us; the launch traced here: 373 us
  waiting for transfers between devices  276 us (74%)
  blocking collectives  34.3 us (9%)
  matrix products  29.7 us (8%)
  between operations  14 us (4%)
  local copies, waits for them, and re-layouts  10.9 us (3%)
  starting transfers between devices  4.86 us (1%)
  other arithmetic  3.85 us (1%)
    all_gather x1, waiting for transfers between devices, on_device(): lax.all_gather(merger_out_w, 'seq', axis=0, tiled=True)  89.4 us
    reduce_scatter x1, waiting for transfers between devices, on_device(): lax.psum_scatter(lax.dot_general(columns, activation, (((0,), (0,)), ((),...  85.8 us
    all_gather x1, waiting for transfers between devices, on_device(): lax.all_gather(merger_in_w, 'seq', axis=1, tiled=True)  83.6 us
    all_gather x1, blocking collectives, on_device(): lax.all_gather(patch_part.astype(jnp.bfloat16), 'grp')  18.7 us
    all_gather x1, blocking collectives, on_device(): wide_rows = lax.all_gather(outgoing, 'grp', axis=2, tiled=True)  15.6 us
    all_to_all x1, waiting for transfers between devices, on_device(): lax.all_to_all(source_grad, 'seq', split_axis=0, concat_axis=0, tiled=True)  11.2 us
    dot_general x1, matrix products, on_device(): jnp.dot(pre_grad, lax.all_gather(merger_in_w, 'seq', axis=1, tiled=True),...  9.68 us
    dot_general x1, matrix products, on_device(): jnp.dot(columns, lax.all_gather(merger_out_w, 'seq', axis=0, tiled=True),...  8.87 us
  transfers between devices with their start and end apart: 5, of which 5 were waited for; matrix products, arithmetic and copies ran while one was open for 12% of the time, Pallas kernels for 0%

profile of v1, /device:TPU:0, one launch (start us, length us, event | category | flops | bytes accessed | tf_op | source)
XLA Modules:
  0.0 373.4 jit_solution(15673111498542636641)
XLA Ops:
  7.2 0.0 copy-start
  7.2 0.0 all-gather.4.cloned.1.call-start
  7.2 0.7 all-gather.4.cloned.1.call-update
  7.9 0.0 all-gather.6.cloned.1.call-start
  8.0 0.7 all-gather.6.cloned.1.call-update
  8.7 0.0 all-gather.8.cloned.1.call-start
  8.7 0.7 all-gather.8.cloned.1.call-update
  9.4 0.8 reshape.495
  10.2 0.8 reshape.496
  10.9 0.8 reshape.497
  11.7 0.1 select_reduce_fusion.2
  11.8 0.1 select_reduce_fusion.1
  12.0 0.1 add_minimum_fusion
  12.0 0.1 compare_and_fusion
  12.1 0.1 min.22
  12.2 0.0 copy-done
  12.2 0.8 gather_fusion
  13.0 0.0 copy-start.1
  13.0 0.2 gather.7
  13.3 0.1 iota_compare_fusion.2
  13.4 0.4 select_select_fusion
  13.8 15.6 %all_gather.16 = bf16[16,3,8192]{2,1,0:T(4,128)(2,1)} all-gather(bf16[16,3,4096]{2,1,0:T(4,128)(2,1)S(1)} %select_select_fusion), channel_id=1, replica_groups=mesh['grp'=2,'seq'=16] {'grp'}, dimensions={2}, use_global_device_ids=true | all-gather | bytes 1179648 | tf_op jit(solution)/shard_map/all_gather | solution.py:82
  29.4 1.7 reshape.498
  31.2 0.0 copy-done.1
  31.2 0.1 convert_reduce_fusion
  31.4 0.3 fusion.31
  31.7 0.1 broadcast_compare_fusion
  31.8 89.4 %all-gather.4.cloned.1.call-done = bf16[8192,1280]{1,0:T(8,128)(2,1)} async-done(((bf16[512,1280]{1,0:T(8,128)(2,1)}), bf16[8192,1280]{1,0:T(8,128)(2,1)}) %all-gather.4.cloned.1.call-update) | async-done | bytes 20971536 | tf_op jit(solution)/shard_map/all_gather | solution.py:87
  121.2 8.9 %convolution_convert_fusion.1 = bf16[48,1280]{1,0:T(8,128)(2,1)S(1)} fusion(bf16[48,8192]{1,0:T(8,128)(2,1)S(1)} %reshape.498, bf16[8192,1280]{1,0:T(8,128)(2,1)} %all-gather.4.cloned.1.call-done), kind=kOutput, calls=%fused_computation.5 | convolution fusion | flops 1006694400 | bytes 21880832 | tf_op jit(solution)/shard_map/dot_general | solution.py:85
  130.0 0.7 reshape.499
  130.8 4.7 %all-to-all-start = ((bf16[16,3,1280]{2,1,0:T(4,128)(2,1)}), bf16[16,3,1280]{2,1,0:T(4,128)(2,1)S(1)}, u32[]{:S(2)}, u32[]{:S(2)}) async-start(bf16[16,3,1280]{2,1,0:T(4,128)(2,1)} %reshape.499), calls=%async_computation | async-start | bytes 327680 | tf_op jit(solution)/shard_map/all_to_all | solution.py:91
  135.5 0.0 reduce-scatter.2.cloned.1.call-start
  135.5 0.3 fusion.69
  135.8 11.2 %all-to-all-done = bf16[16,3,1280]{2,1,0:T(4,128)(2,1)S(1)} async-done(((bf16[16,3,1280]{2,1,0:T(4,128)(2,1)}), bf16[16,3,1280]{2,1,0:T(4,128)(2,1)S(1)}, u32[]{:S(2)}, u32[]{:S(2)}) %all-to-all-start) | async-done | bytes 122912 | tf_op jit(solution)/shard_map/all_to_all | solution.py:91
  147.0 0.1 reshape.504
  147.1 83.6 %all-gather.6.cloned.1.call-done = bf16[1280,5120]{0,1:T(8,128)(2,1)} async-done(((bf16[1280,320]{0,1:T(8,128)(2,1)}), bf16[1280,5120]{0,1:T(8,128)(2,1)}) %all-gather.6.cloned.1.call-update) | async-done | bytes 13107216 | tf_op jit(solution)/shard_map/all_gather | solution.py:97
  230.6 9.7 %fusion.55 = f32[48,5120]{1,0:T(8,128)} fusion(bf16[1280,5120]{0,1:T(8,128)(2,1)} %all-gather.6.cloned.1.call-done, f32[48,1280]{1,0:T(8,128)S(1)} %reshape.504, bf16[48,1,1280]{2,0,1:T(8,128)(2,1)} %param.15), kind=kOutput, calls=%fused_computation.70 | convolution fusion | flops 629821440 | bytes 14458880 | tf_op jit(solution)/shard_map/dot_general | solution.py:95
  240.3 2.5 reshape.500
  242.9 0.0 copy-start.3
  242.9 2.1 convolution_convert_fusion
  245.0 0.9 convert_element_type.89
  245.9 18.7 %all_gather.19 = bf16[2,192,1280]{2,1,0:T(8,128)(2,1)} all-gather(bf16[1,192,1280]{2,1,0:T(8,128)(2,1)} %convert_element_type.89), channel_id=1, replica_groups=mesh['grp'=2,'seq'=16] {'grp'}, dimensions={0}, use_global_device_ids=true | all-gather | bytes 1474560 | tf_op jit(solution)/shard_map/all_gather | solution.py:108
  264.5 1.4 reduce_sum.90
  265.9 0.0 copy-done.3
  266.0 0.3 fusion.4
  266.3 5.2 %fusion.35 = f32[1280,1280]{1,0:T(8,128)} fusion(bf16[192,1,1280]{2,0,1:T(8,128)(2,1)} %param.17, bf16[192,1280]{1,0:T(8,128)(2,1)S(1)} %reduce_sum.90, bf16[192,1,1280]{2,0,1:T(8,128)(2,1)S(1)} %copy-done.1, f32[192]{0:T(256)S(1)} %broadcast_multiply_fusion, f32[192]{0:T(256)S(1)} %broadcast_multiply_fusion.2, f32[192]{0:T(256)S(1)} %broadcast_multiply_fusion.1, ...), kind=kOutput, calls=%fused_computation.47 | convolution fusion | flops 633323520 | bytes 8036352 | tf_op jit(solution)/shard_map/dot_general | solution.py:132
  271.5 0.0 reduce-scatter.2.cloned.1.call-update
  271.6 0.4 fusion.19
  272.0 0.0 copy-start.2
  272.0 0.8 copy-done.2
  272.7 0.7 dynamic-slice_bitcast_fusion
  273.5 3.8 %all-gather.8.cloned.1.call-done = bf16[1280,1280]{1,0:T(8,128)(2,1)} async-done(((bf16[80,1280]{1,0:T(8,128)(2,1)}), bf16[1280,1280]{1,0:T(8,128)(2,1)}) %all-gather.8.cloned.1.call-update) | async-done | bytes 3276816 | tf_op jit(solution)/shard_map/all_gather | solution.py:121
  277.3 3.8 %fusion.1 = bf16[192,1,1280]{2,0,1:T(8,128)(2,1)} fusion(bf16[192,1280]{1,0:T(8,128)(2,1)} %copy-done.2, bf16[1280,1280]{1,0:T(8,128)(2,1)} %all-gather.8.cloned.1.call-done, bf16[192,1,1280]{2,0,1:T(8,128)(2,1)} %param.17), kind=kOutput, calls=%fused_computation.4 | convolution fusion | flops 631848960 | bytes 4751360 | tf_op jit(solution)/shard_map/dot_general | solution.py:119
  281.1 85.8 %reduce-scatter.2.cloned.1.call-done = f32[80,1280]{1,0:T(8,128)} async-done(((f32[1280,1280]{1,0:T(8,128)}), f32[80,1280]{1,0:T(8,128)}) %reduce-scatter.2.cloned.1.call-update) | async-done | bytes 409616 | tf_op jit(solution)/shard_map/reduce_scatter | solution.py:131
  (12 shorter events, 0.1 us)
Async XLA Ops:
  7.2 5.1 %copy-start = (bf16[256,4096]{1,0:T(8,128)(2,1)S(1)}, bf16[256,4096]{1,0:T(8,128)(2,1)}, u32[]{:S(2)}) copy-start(bf16[256,4096]{1,0:T(8,128)(2,1)} %param.11) | copy-start | bytes 6291460
  7.2 114.0 %all-gather.4.cloned.1.call-start = ((), (), s32[]{:S(2)}) async-start(), calls=%async_computation.2 | async-start | bytes 22282240 | tf_op jit(solution)/shard_map/all_gather | solution.py:87
  7.9 222.7 %all-gather.6.cloned.1.call-start = ((), (), s32[]{:S(2)}) async-start(), calls=%async_computation.3 | async-start | bytes 13926400 | tf_op jit(solution)/shard_map/all_gather | solution.py:97
  8.7 268.6 %all-gather.8.cloned.1.call-start = ((), (), s32[]{:S(2)}) async-start(), calls=%async_computation.4 | async-start | bytes 3481600 | tf_op jit(solution)/shard_map/all_gather | solution.py:121
  13.0 18.2 %copy-start.1 = (bf16[192,1,1280]{2,0,1:T(8,128)(2,1)S(1)}, bf16[192,1,1280]{2,0,1:T(8,128)(2,1)}, u32[]{:S(2)}) copy-start(bf16[192,1,1280]{2,0,1:T(8,128)(2,1)} %param.16) | copy-start | bytes 1474564
  130.8 16.2 %all-to-all-start = ((bf16[16,3,1280]{2,1,0:T(4,128)(2,1)}), bf16[16,3,1280]{2,1,0:T(4,128)(2,1)S(1)}, u32[]{:S(2)}, u32[]{:S(2)}) async-start(bf16[16,3,1280]{2,1,0:T(4,128)(2,1)} %reshape.499), calls=%async_computation | async-start | bytes 327680 | tf_op jit(solution)/shard_map/all_to_all | solution.py:91
  135.5 231.4 %reduce-scatter.2.cloned.1.call-start = ((), (), s32[]{:S(2)}) async-start(), calls=%async_computation.5 | async-start | bytes 6963200 | tf_op jit(solution)/shard_map/reduce_scatter | solution.py:131
  242.9 23.1 %copy-start.3 = (f32[1280]{0:T(1024)S(1)}, f32[1280]{0:T(1024)}, u32[]{:S(2)}) copy-start(f32[1280]{0:T(1024)} %param.18) | copy-start | bytes 15364
  272.0 0.8 copy-start.2
Sparse Core Ops, SparseCore 0:
  9.6 111.5 all-gather.3
  123.4 107.1 all-gather.5
  232.9 44.2 all-gather.7
  281.7 85.1 reduce-scatter.1
